TPU v7x, 32 devices: a whole 2x2x4 slice. The times are simulated.
32 devices in a mesh: grp: 2 (over y), tp: 8 (over z, x), sub: 2 (over core).
Axes of the slice: x: 2, y: 2, z: 4, core: 2. Of those that a mesh axis runs over, the one named last changes fastest.
Arguments:
- hidden_in: bfloat16 [32, 2, 4096], P('grp', 'sub', 'tp'), parts along dimension 0, may hold values from -16 to 16
- norm_attn: float32 [8192], replicated, may hold values from 0.25 to 1.75
- w_query: bfloat16 [8192, 2, 4096], P(None, 'sub', 'tp'), may hold values from -0.0625 to 0.0625
- w_key: bfloat16 [8192, 2, 512], P(None, 'sub', 'tp'), may hold values from -0.0625 to 0.0625
- w_value: bfloat16 [8192, 2, 512], P(None, 'sub', 'tp'), may hold values from -0.0625 to 0.0625
- w_out: bfloat16 [2, 4096, 2, 4096], P('sub', None, None, 'tp'), may hold values from -0.0625 to 0.0625
- norm_ffn: float32 [8192], replicated, may hold values from 0.25 to 1.75
- w_gate: bfloat16 [2, 4096, 14336], P('sub', None, 'tp'), may hold values from -0.0625 to 0.0625
- w_up: bfloat16 [2, 4096, 14336], P('sub', None, 'tp'), may hold values from -0.0625 to 0.0625
- w_down: bfloat16 [14336, 2, 4096], P('tp', 'sub'), may hold values from -0.0625 to 0.0625
- cache_keys: bfloat16 [32, 64, 8, 128], P('grp', 'tp', 'sub'), parts along dimension 0, may hold values from -250 to 250
- cache_values: bfloat16 [32, 64, 8, 128], P('grp', 'tp', 'sub'), parts along dimension 0, may hold values from -6 to 6
- lengths: int32 [32], P('grp'), parts along dimension 0, may hold values from 1 to 64, as said below
Outputs:
- hidden_out: bfloat16 [32, 2, 4096], P('grp', 'sub', 'tp'), parts along dimension 0
There are 2 independent parts, one for each index of `grp`. A program takes and returns all parts, laid end to end along the dimension named above; an argument that names none is the same for every part. Nothing has to cross between parts.
Inputs may be any that keep to these rules, and one draw needn't show every extreme that they name: `lengths`: some sequence has 64 live positions and some has 1.
All inputs are finite; a program needn't handle non-finite values.
Results may differ from a plain program's by a relative error of at most 0.012.
The roundings to bfloat16 on the way count: a program that leaves them out, or rounds other values in their place, can miss the bound.
Values may be sent and summed in bfloat16 or wider, within the bound.
A program may use at most 128 MiB of HBM per device.

v0:
```python
import math
import jax
import jax.numpy as jnp
from jax import lax
from jax.sharding import PartitionSpec as P

HD = 128
epsilon = 1e-05
rope_base = 500000.0
floor_score = -1e30


def joined(part, axis, combine):
    gathered = jax.tree.map(lambda a: lax.all_gather(a, axis), part)

    def take(source):
        return jax.tree.map(lambda a: lax.dynamic_index_in_dim(a, source, 0, False), gathered)

    return lax.fori_loop(
        1, lax.axis_size(axis), lambda source, state: combine(state, take(source)), take(0)
    )


def rope_angles(lengths):
    frequencies = rope_base ** (-(jnp.arange(HD // 2, dtype=jnp.float32) * 2.0) / HD)
    return lengths.astype(jnp.float32)[:, None] * frequencies[None, :]


def rotate(vectors, angles):
    middle_index = vectors.shape[-1] // 2
    cosine = jnp.cos(angles)[:, None, :]
    sine = jnp.sin(angles)[:, None, :]
    lower = vectors[..., :middle_index]
    upper = vectors[..., middle_index:]
    return jnp.concatenate([lower * cosine - upper * sine, upper * cosine + lower * sine], axis=-1)


def spread_rows(shard):
    across = lax.all_gather(shard, "tp", axis=2, tiled=True)
    return lax.all_gather(across, "sub", axis=1, tiled=True)


def half_rows_of(shard):
    return lax.all_gather(shard, "tp", axis=2, tiled=True)


def join_partials(earlier, later):
    earlier_max, earlier_sum, earlier_out = earlier
    later_max, later_sum, later_out = later
    highest = jnp.maximum(earlier_max, later_max)
    earlier_scale = jnp.exp(earlier_max - highest)
    later_scale = jnp.exp(later_max - highest)
    joined_sum = earlier_sum * earlier_scale + later_sum * later_scale
    joined_out = earlier_out * earlier_scale[..., None] + later_out * later_scale[..., None]
    return (highest, joined_sum, joined_out)


def per_device(
    hidden_in,
    norm_attn,
    w_query,
    w_key,
    w_value,
    w_out,
    norm_ffn,
    w_gate,
    w_up,
    w_down,
    cache_keys,
    cache_values,
    lengths,
):
    seq_count = hidden_in.shape[0]
    shard_width = hidden_in.shape[2]
    half_width = shard_width * lax.axis_size("tp")
    model_width = half_width * lax.axis_size("sub")
    tp_pos = lax.axis_index("tp")
    sub_pos = lax.axis_index("sub")
    residual = hidden_in.astype(jnp.float32)
    whole_rows = spread_rows(hidden_in).astype(jnp.float32)
    factor = lax.rsqrt(jnp.mean(whole_rows * whole_rows, axis=(1, 2)) + epsilon)
    gain_whole = norm_attn.reshape(whole_rows.shape[1], half_width)
    gathered = (whole_rows * factor[:, None, None] * gain_whole).astype(jnp.bfloat16)
    flattened = gathered.reshape(seq_count, model_width)
    query_part = jnp.dot(
        flattened, w_query.reshape(model_width, -1), preferred_element_type=jnp.float32
    ).astype(jnp.bfloat16)
    key_part = jnp.dot(
        flattened, w_key.reshape(model_width, -1), preferred_element_type=jnp.float32
    ).astype(jnp.bfloat16)
    value_part = jnp.dot(
        flattened, w_value.reshape(model_width, -1), preferred_element_type=jnp.float32
    ).astype(jnp.bfloat16)
    query, key_new, value_new = (
        lax.all_gather(query_part, "tp", axis=1, tiled=True),
        lax.all_gather(key_part, "tp", axis=1, tiled=True),
        lax.all_gather(value_part, "tp", axis=1, tiled=True),
    )
    query_heads = query.shape[1] // HD
    kv_heads = key_new.shape[1] // HD
    group_size = query_heads // kv_heads
    angles = rope_angles(lengths)
    query_rot = rotate(
        query.astype(jnp.float32).reshape(seq_count, query_heads, HD), angles
    ).astype(jnp.bfloat16)
    key_rot = rotate(key_new.astype(jnp.float32).reshape(seq_count, kv_heads, HD), angles).astype(
        jnp.bfloat16
    )
    grouped = query_rot.reshape(seq_count, kv_heads, group_size, HD)
    values_new = value_new.astype(jnp.float32).reshape(seq_count, kv_heads, 1, HD)
    span = cache_keys.shape[1]
    scores = jnp.einsum(
        "bkgd,blkd->bkgl", grouped, cache_keys, preferred_element_type=jnp.float32
    ) / math.sqrt(HD)
    places = tp_pos * span + jnp.arange(span, dtype=jnp.int32)
    live = (places[None, :] < lengths[:, None])[:, None, None, :]
    masked = jnp.where(live, scores, floor_score)
    local_max = jnp.max(masked, axis=-1)
    weights = jnp.where(live, jnp.exp(masked - local_max[..., None]), 0.0)
    local_sum = jnp.sum(weights, axis=-1)
    local_out = jnp.einsum(
        "bkgl,blkd->bkgd",
        weights,
        cache_values.astype(jnp.float32),
        precision=lax.Precision.HIGHEST,
    )
    own_score = jnp.sum(
        grouped.astype(jnp.float32) * key_rot.astype(jnp.float32)[:, :, None, :], axis=-1
    ) / math.sqrt(HD)
    joined_max, joined_sum, joined_out = joined(
        (local_max, local_sum, local_out), "tp", join_partials
    )
    highest = jnp.maximum(joined_max, own_score)
    kept_scale = jnp.exp(joined_max - highest)
    own_weight = jnp.exp(own_score - highest)
    numerator = joined_out * kept_scale[..., None] + own_weight[..., None] * values_new
    denominator = joined_sum * kept_scale + own_weight
    attended = (numerator / denominator[..., None]).reshape(seq_count, -1).astype(jnp.bfloat16)
    out_part = jnp.dot(
        attended, w_out.reshape(attended.shape[1], -1), preferred_element_type=jnp.float32
    )
    out_part = out_part.reshape(seq_count, -1, shard_width)
    mixed = lax.psum_scatter(out_part, "sub", scatter_dimension=1, tiled=True)
    middle = (residual + mixed).astype(jnp.bfloat16)
    middle_float = middle.astype(jnp.float32)
    raw_half = half_rows_of(middle).astype(jnp.float32)
    partial_squares = jnp.sum(raw_half * raw_half, axis=(1, 2))
    squares_mid = lax.psum(partial_squares, "sub")
    factor_mid = lax.rsqrt(squares_mid / model_width + epsilon)
    gain_half = lax.dynamic_slice_in_dim(norm_ffn, sub_pos * half_width, half_width)
    half_rows = (raw_half * factor_mid[:, None, None] * gain_half).astype(jnp.bfloat16)
    half_flat = half_rows.reshape(seq_count, half_width)
    gate_part = jnp.dot(
        half_flat, w_gate.reshape(half_width, -1), preferred_element_type=jnp.float32
    )
    up_part = jnp.dot(half_flat, w_up.reshape(half_width, -1), preferred_element_type=jnp.float32)
    gate_total, up_total = lax.psum((gate_part, up_part), "sub")
    hidden = (jax.nn.silu(gate_total) * up_total).astype(jnp.bfloat16)
    down_part = jnp.dot(
        hidden, w_down.reshape(hidden.shape[1], -1), preferred_element_type=jnp.float32
    )
    down_total = lax.psum(down_part, "tp")
    down_share = lax.dynamic_slice_in_dim(down_total, tp_pos * shard_width, shard_width, 1)
    return (middle_float + down_share[:, None, :]).astype(jnp.bfloat16)


def solution(mesh):
    in_specs = (
        P("grp", "sub", "tp"),
        P(),
        P(None, "sub", "tp"),
        P(None, "sub", "tp"),
        P(None, "sub", "tp"),
        P("sub", None, None, "tp"),
        P(),
        P("sub", None, "tp"),
        P("sub", None, "tp"),
        P("tp", "sub", None),
        P("grp", "tp", "sub", None),
        P("grp", "tp", "sub", None),
        P("grp"),
    )
    out_specs = P("grp", "sub", "tp")
    return jax.shard_map(
        per_device, mesh=mesh, in_specs=in_specs, out_specs=out_specs, check_vma=False
    )
```

profile of v0, /device:TPU:0, one launch (start us, length us, event | category | flops | bytes accessed | tf_op | source)
XLA Modules:
  0.0 410.7 jit_solution(6426538400944346462)
XLA Ops:
  6.6 32.7 %all_gather.36 = bf16[16,1,4096]{2,0,1:T(8,128)(2,1)S(1)} all-gather(bf16[16,1,512]{2,0,1:T(8,128)(2,1)} %param.15), channel_id=1, replica_groups=mesh['grp'=2,'tp'=8,'sub'=2] {'tp'}, dimensions={2}, use_global_device_ids=true | all-gather | bytes 147456 | tf_op jit(solution)/shard_map/all_gather | solution.py:39
  39.3 2.0 all_gather.37
  41.5 0.8 mul.255
  42.4 4.6 %fusion.12 = bf16[16,512]{1,0:T(8,128)(2,1)S(1)} fusion(bf16[16,8192]{1,0:T(8,128)(2,1)S(1)} %bitcast.90, bf16[8192,1,512]{2,0,1:T(8,128)(2,1)} %param.17), kind=kOutput, calls=%fused_computation.18 | convolution fusion | flops 134225920 | bytes 8667136 | tf_op jit(solution)/shard_map/dot_general | solution.py:85
  47.0 30.5 %all_gather.38 = bf16[16,4096]{1,0:T(8,128)(2,1)S(1)} all-gather(bf16[16,512]{1,0:T(8,128)(2,1)S(1)} %fusion.12), channel_id=1, replica_groups=mesh['grp'=2,'tp'=8,'sub'=2] {'tp'}, dimensions={1}, use_global_device_ids=true | all-gather | bytes 147456 | tf_op jit(solution)/shard_map/all_gather | solution.py:95
  78.3 1.3 fusion.26
  79.9 31.0 %all-gather.1 = f32[128,4,8]{2,1,0:T(4,128)S(1)} all-gather(f32[16,4,8]{2,1,0:T(4,128)S(1)} %fusion.27), channel_id=3, replica_groups=mesh['grp'=2,'tp'=8,'sub'=2] {'tp'}, dimensions={0}, use_global_device_ids=true | all-gather | bytes 18432 | tf_op jit(solution)/shard_map/all_gather | solution.py:14
  111.1 31.7 %all-gather = f32[128,4,8]{2,1,0:T(4,128)S(1)} all-gather(f32[16,4,8]{2,1,0:T(4,128)S(1)} %get-tuple-element.236), channel_id=2, replica_groups=mesh['grp'=2,'tp'=8,'sub'=2] {'tp'}, dimensions={0}, use_global_device_ids=true | all-gather | bytes 18432 | tf_op jit(solution)/shard_map/all_gather | solution.py:14
  143.4 30.6 %all-gather.3 = bf16[8,64,16]{1,2,0:T(8,128)(2,1)S(1)} all-gather(bf16[1,64,16]{1,2,0:T(8,128)(2,1)S(1)} %fusion.15), channel_id=1, replica_groups=mesh['grp'=2,'tp'=8,'sub'=2] {'tp'}, dimensions={0}, use_global_device_ids=true | all-gather | bytes 18432 | tf_op jit(solution)/shard_map/all_gather | solution.py:96
  175.1 30.6 %all-gather.4 = bf16[8,64,16]{1,2,0:T(8,128)(2,1)S(1)} all-gather(bf16[1,64,16]{1,2,0:T(8,128)(2,1)S(1)} %fusion.16), channel_id=1, replica_groups=mesh['grp'=2,'tp'=8,'sub'=2] {'tp'}, dimensions={0}, use_global_device_ids=true | all-gather | bytes 18432 | tf_op jit(solution)/shard_map/all_gather | solution.py:97
  205.8 9.3 %copy.83 = bf16[512,8,2,512]{3,1,2,0:T(8,128)(2,1)} copy(bf16[512,8,2,512]{3,2,1,0:T(2,128)(2,1)} %bitcast.89) | data formatting | bytes 16777216
  215.1 11.4 %copy.75 = bf16[1024,4096]{1,0:T(8,128)(2,1)} copy(bf16[1024,4096]{0,1:T(8,128)(2,1)} %bitcast.88) | data formatting | bytes 16777216 | tf_op jit(solution)/shard_map/dot_general | solution.py:139
  226.5 1.0 slice.26
  227.5 10.0 %while.19 = (s32[]{:T(128)}, f32[16,4,8]{0,2,1:T(8,128)S(1)}, f32[16,4,8]{0,2,1:T(8,128)S(1)}, f32[16,4,8,128]{3,2,1,0:T(8,128)S(1)}, f32[8,16,4,8]{1,3,2,0:T(8,...) while((s32[]{:T(128)}, f32[16,4,8]{0,2,1:T(8,128)S(1)}, ...), condition=%wide.region_4.5_spmd, body=%wide.region_3.4_spmd.sunk | while | flops 199685 | bytes 815255 | solution.py:19
  227.7 1.2 fusion.58
  229.1 1.2 fusion.58
  230.5 1.2 fusion.58
  231.9 1.2 fusion.58
  233.4 1.2 fusion.58
  234.8 1.2 fusion.58
  236.2 1.2 fusion.58
  238.1 6.3 %fusion.49 = f32[16,2,512]{2,0,1:T(8,128)} fusion(bf16[16,4096,1]{1,0,2:T(8,128)(2,1)S(1)} %reshape.198, bf16[2,512,4096]{2,1,0:T(8,128)(2,1)} %bitcast.87), kind=kOutput, calls=%fused_computation.77 | convolution fusion | flops 134217728 | bytes 8585216 | tf_op jit(solution)/shard_map/dot_general | solution.py:139
  244.5 8.5 %reduce-scatter.2.cloned.1.call-done = f32[16,1,512]{2,0,1:T(8,128)} async-done(((f32[16,2,512]{2,0,1:T(8,128)}), f32[16,1,512]{2,0,1:T(8,128)}) %reduce-scatter.2.cloned.1.call-update) | async-done | bytes 32784 | tf_op jit(solution)/shard_map/reduce_scatter | solution.py:143
  253.0 0.8 add_convert_fusion.1
  253.8 30.8 %all_gather.47 = bf16[16,1,4096]{2,0,1:T(8,128)(2,1)S(1)} all-gather(bf16[16,1,512]{2,0,1:T(8,128)(2,1)S(1)} %add_convert_fusion.1), channel_id=1, replica_groups=mesh['grp'=2,'tp'=8,'sub'=2] {'tp'}, dimensions={2}, use_global_device_ids=true | all-gather | bytes 147456 | tf_op jit(solution)/shard_map/all_gather | solution.py:44
  284.7 2.6 psum.28
  287.3 7.9 %fusion.7 = f32[16,1792]{1,0:T(8,128)} fusion(bf16[1,4096,1792]{2,1,0:T(8,128)(2,1)} %param.22, bf16[16,1,4096]{2,0,1:T(8,128)(2,1)S(1)} %all_gather.47, f32[4096]{0:T(1024)S(1)} %dynamic_slice.50, f32[16]{0:T(128)S(1)} %add_rsqrt_fusion), kind=kOutput, calls=%fused_computation.12 | convolution fusion | flops 235143168 | bytes 14942272 | tf_op jit(solution)/shard_map/dot_general | solution.py:153
  295.2 7.9 %fusion.5 = f32[16,1792]{1,0:T(8,128)} fusion(bf16[1,4096,1792]{2,1,0:T(8,128)(2,1)} %param.23, bf16[16,1,4096]{2,0,1:T(8,128)(2,1)S(1)} %all_gather.47, f32[4096]{0:T(1024)S(1)} %dynamic_slice.50, f32[16]{0:T(128)S(1)} %add_rsqrt_fusion), kind=kOutput, calls=%fused_computation.10 | convolution fusion | flops 235143168 | bytes 14942272 | tf_op jit(solution)/shard_map/dot_general | solution.py:156
  303.2 19.1 %all-reduce.6.cloned.1.call-done = (f32[16,1792]{1,0:T(8,128)}, f32[16,1792]{1,0:T(8,128)}) async-done(((f32[16,1792]{1,0:T(8,128)}, f32[16,1792]{1,0:T(8,128)}), (f32[16,1792]{1,0:T(8,128)}, f32[16,1792]{1,0:T(8,128)})) %all-reduce.6.cloned.1.call-update) | async-done | bytes 229392 | tf_op jit(solution)/shard_map/psum | solution.py:157
  322.4 8.0 %fusion.3 = f32[16,4096]{1,0:T(8,128)} fusion(bf16[1792,1,4096]{2,0,1:T(8,128)(2,1)} %param.24, f32[16,1792]{1,0:T(8,128)} %get-tuple-element.221, f32[16,1792]{1,0:T(8,128)} %get-tuple-element.222), kind=kOutput, calls=%fused_computation.8 | convolution fusion | flops 235053056 | bytes 15171584 | tf_op jit(solution)/shard_map/dot_general | solution.py:159
  330.4 72.4 %all-reduce.4.cloned.1.call-done = f32[16,4096]{1,0:T(8,128)} async-done(((f32[16,4096]{1,0:T(8,128)}), f32[16,4096]{1,0:T(8,128)}) %all-reduce.4.cloned.1.call-update) | async-done | bytes 262160 | tf_op jit(solution)/shard_map/psum | solution.py:162
  402.8 1.4 fusion.37
  (87 shorter events, 5.4 us)
Async XLA Ops:
  6.5 136.5 %copy-start = (bf16[8192,1,64]{0,2,1:T(8,128)(2,1)S(1)}, bf16[8192,1,64]{0,2,1:T(8,128)(2,1)}, u32[]{:S(2)}) copy-start(bf16[8192,1,64]{0,2,1:T(8,128)(2,1)} %param.18) | copy-start | bytes 3145732
  6.5 71.1 %copy-start.7 = (s32[16]{0:T(128)S(1)}, s32[16]{0:T(128)}, u32[]{:S(2)}) copy-start(s32[16]{0:T(128)} %param.27) | copy-start | bytes 196
  6.5 71.4 %copy-start.3 = (bf16[16,8,4,128]{3,2,1,0:T(4,128)(2,1)S(1)}, bf16[16,8,4,128]{3,2,1,0:T(4,128)(2,1)}, u32[]{:S(2)}) copy-start(bf16[16,8,4,128]{3,2,1,0:T(4,128)(2,1)} %param.25) | copy-start | bytes 393220
  6.5 71.8 %copy-start.4 = (bf16[16,8,4,128]{3,2,1,0:T(4,128)(2,1)S(1)}, bf16[16,8,4,128]{3,2,1,0:T(4,128)(2,1)}, u32[]{:S(2)}) copy-start(bf16[16,8,4,128]{3,2,1,0:T(4,128)(2,1)} %param.26) | copy-start | bytes 393220
  6.5 168.1 %copy-start.2 = (bf16[8192,1,64]{0,2,1:T(8,128)(2,1)S(1)}, bf16[8192,1,64]{0,2,1:T(8,128)(2,1)}, u32[]{:S(2)}) copy-start(bf16[8192,1,64]{0,2,1:T(8,128)(2,1)} %param.19) | copy-start | bytes 3145732
  6.5 219.9 %all-gather.7.cloned.1.call-start = ((), (), s32[]{:S(2)}) async-start(), calls=%async_computation.3 | async-start | bytes 2359296 | tf_op jit(solution)/shard_map/all_gather | solution.py:14
  79.7 173.3 %reduce-scatter.2.cloned.1.call-start = ((), (), s32[]{:S(2)}) async-start(), calls=%async_computation.1 | async-start | bytes 98304 | tf_op jit(solution)/shard_map/reduce_scatter | solution.py:143
  215.1 29.3 %copy-start.6 = (f32[8192]{0:T(1024)S(1)}, f32[8192]{0:T(1024)}, u32[]{:S(2)}) copy-start(f32[8192]{0:T(1024)} %param.21) | copy-start | bytes 98308
  215.1 37.9 %copy-start.5 = (bf16[16,1,512]{2,0,1:T(8,128)(2,1)S(1)}, bf16[16,1,512]{2,0,1:T(8,128)(2,1)}, u32[]{:S(2)}) copy-start(bf16[16,1,512]{2,0,1:T(8,128)(2,1)} %param.15) | copy-start | bytes 49156
  244.4 78.0 %all-reduce.6.cloned.1.call-start = ((), (), s32[]{:S(2)}) async-start(), calls=%async_computation.4 | async-start | bytes 458752 | tf_op jit(solution)/shard_map/psum | solution.py:157
  295.2 109.0 %copy-start.1 = (bf16[8192,1,64]{0,2,1:T(8,128)(2,1)S(1)}, bf16[8192,1,64]{0,2,1:T(8,128)(2,1)}, u32[]{:S(2)}) copy-start(bf16[8192,1,64]{0,2,1:T(8,128)(2,1)} %param.18) | copy-start | bytes 3145732
  303.2 99.6 %all-reduce.4.cloned.1.call-start = ((), (), s32[]{:S(2)}) async-start(), calls=%async_computation.2 | async-start | bytes 524288 | tf_op jit(solution)/shard_map/psum | solution.py:162
Sparse Core Ops, SparseCore 0:
  79.8 53.2 all-gather.6
  244.5 8.4 reduce-scatter.1
  303.3 19.0 all-reduce.5
  330.5 72.2 all-reduce.3
where the time goes:
time: 412 us; the launch traced here: 411 us
  blocking collectives  223 us (54%)
  waiting for transfers between devices  100 us (24%)
  matrix products  37.1 us (9%)
  local copies, waits for them, and re-layouts  24.6 us (6%)
  between operations  13.3 us (3%)
  other arithmetic  12.6 us (3%)
    psum x1, waiting for transfers between devices, per_device(): down_total = lax.psum(down_part, 'tp')  72.4 us
    all_gather x2, blocking collectives, joined(): gathered = jax.tree.map(lambda a: lax.all_gather(a, axis), part)  62.7 us
    all_gather x1, blocking collectives, spread_rows(): across = lax.all_gather(shard, 'tp', axis=2, tiled=True)  32.7 us
    all_gather x1, blocking collectives, half_rows_of(): return lax.all_gather(shard, 'tp', axis=2, tiled=True)  30.8 us
    all_gather x1, blocking collectives, per_device(): lax.all_gather(key_part, 'tp', axis=1, tiled=True)  30.6 us
    all_gather x1, blocking collectives, per_device(): lax.all_gather(value_part, 'tp', axis=1, tiled=True)  30.6 us
    all_gather x1, blocking collectives, per_device(): lax.all_gather(query_part, 'tp', axis=1, tiled=True)  30.5 us
    psum x1, waiting for transfers between devices, per_device(): gate_total, up_total = lax.psum((gate_part, up_part), 'sub')  19.1 us
  transfers between devices with their start and end apart: 4, of which 3 were waited for; matrix products, arithmetic and copies ran while one was open for 6% of the time, Pallas kernels for 0%

commit v1 on v0

--- a/solution.py
+++ b/solution.py
@@ -8,6 +8,10 @@
 epsilon = 1e-05
 rope_base = 500000.0
 floor_score = -1e30
+
+
+def divide_ends_on_mesh(net_axis, vals):
+    return lax.all_gather(vals, axis_name=net_axis).sum(axis=0)
 
 
 def joined(part, axis, combine):
@@ -159,7 +163,7 @@
     down_part = jnp.dot(
         hidden, w_down.reshape(hidden.shape[1], -1), preferred_element_type=jnp.float32
     )
-    down_total = lax.psum(down_part, "tp")
+    down_total = divide_ends_on_mesh("tp", down_part)
     down_share = lax.dynamic_slice_in_dim(down_total, tp_pos * shard_width, shard_width, 1)
     return (middle_float + down_share[:, None, :]).astype(jnp.bfloat16)
 

time: 412 us -> 391 us (0.949)
  waiting for transfers between devices: 100 us -> 78.2 us
    psum x1 -> x0, waiting for transfers between devices: 72.4 us -> none  [per_device(): down_total = lax.psum(down_part, 'tp')]
    all_gather x0 -> x1, waiting for transfers between devices: none -> 50.5 us  [divide_ends_on_mesh(): return lax.all_gather(vals, axis_name=net_axis).sum(axis=0)]
where the time goes in v1:
time: 391 us; the launch traced here: 390 us
  blocking collectives  223 us (57%)
  waiting for transfers between devices  78.2 us (20%)
  matrix products  37.2 us (10%)
  local copies, waits for them, and re-layouts  24.6 us (6%)
  other arithmetic  13.5 us (3%)
  between operations  13.4 us (3%)
    all_gather x2, blocking collectives, joined(): gathered = jax.tree.map(lambda a: lax.all_gather(a, axis), part)  62.7 us
    all_gather x1, waiting for transfers between devices, divide_ends_on_mesh(): return lax.all_gather(vals, axis_name=net_axis).sum(axis=0)  50.5 us
    all_gather x1, blocking collectives, spread_rows(): across = lax.all_gather(shard, 'tp', axis=2, tiled=True)  32.7 us
    all_gather x1, blocking collectives, half_rows_of(): return lax.all_gather(shard, 'tp', axis=2, tiled=True)  30.8 us
    all_gather x1, blocking collectives, per_device(): lax.all_gather(key_part, 'tp', axis=1, tiled=True)  30.6 us
    all_gather x1, blocking collectives, per_device(): lax.all_gather(value_part, 'tp', axis=1, tiled=True)  30.6 us
    all_gather x1, blocking collectives, per_device(): lax.all_gather(query_part, 'tp', axis=1, tiled=True)  30.5 us
    psum x1, waiting for transfers between devices, per_device(): gate_total, up_total = lax.psum((gate_part, up_part), 'sub')  19.1 us
  transfers between devices with their start and end apart: 4, of which 3 were waited for; matrix products, arithmetic and copies ran while one was open for 6% of the time, Pallas kernels for 0%

profile of v1, /device:TPU:0, one launch (start us, length us, event | category | flops | bytes accessed | tf_op | source)
XLA Modules:
  0.0 389.9 jit_solution(7088242958804928806)
XLA Ops:
  6.6 32.7 %all_gather.42 = bf16[16,1,4096]{2,0,1:T(8,128)(2,1)S(1)} all-gather(bf16[16,1,512]{2,0,1:T(8,128)(2,1)} %param.15), channel_id=1, replica_groups=mesh['grp'=2,'tp'=8,'sub'=2] {'tp'}, dimensions={2}, use_global_device_ids=true | all-gather | bytes 147456 | tf_op jit(solution)/shard_map/all_gather | solution.py:43
  39.2 2.0 all_gather.43
  41.4 0.8 mul.255
  42.4 4.7 %fusion.12 = bf16[16,512]{1,0:T(8,128)(2,1)S(1)} fusion(bf16[16,8192]{1,0:T(8,128)(2,1)S(1)} %bitcast.91, bf16[8192,1,512]{2,0,1:T(8,128)(2,1)} %param.17), kind=kOutput, calls=%fused_computation.18 | convolution fusion | flops 134225920 | bytes 8667136 | tf_op jit(solution)/shard_map/dot_general | solution.py:89
  47.1 30.5 %all_gather.44 = bf16[16,4096]{1,0:T(8,128)(2,1)S(1)} all-gather(bf16[16,512]{1,0:T(8,128)(2,1)S(1)} %fusion.12), channel_id=1, replica_groups=mesh['grp'=2,'tp'=8,'sub'=2] {'tp'}, dimensions={1}, use_global_device_ids=true | all-gather | bytes 147456 | tf_op jit(solution)/shard_map/all_gather | solution.py:99
  78.4 1.3 fusion.26
  80.0 31.0 %all-gather.1 = f32[128,4,8]{2,1,0:T(4,128)S(1)} all-gather(f32[16,4,8]{2,1,0:T(4,128)S(1)} %fusion.27), channel_id=3, replica_groups=mesh['grp'=2,'tp'=8,'sub'=2] {'tp'}, dimensions={0}, use_global_device_ids=true | all-gather | bytes 18432 | tf_op jit(solution)/shard_map/all_gather | solution.py:18
  111.2 31.7 %all-gather = f32[128,4,8]{2,1,0:T(4,128)S(1)} all-gather(f32[16,4,8]{2,1,0:T(4,128)S(1)} %get-tuple-element.236), channel_id=2, replica_groups=mesh['grp'=2,'tp'=8,'sub'=2] {'tp'}, dimensions={0}, use_global_device_ids=true | all-gather | bytes 18432 | tf_op jit(solution)/shard_map/all_gather | solution.py:18
  143.5 30.6 %all-gather.4 = bf16[8,64,16]{1,2,0:T(8,128)(2,1)S(1)} all-gather(bf16[1,64,16]{1,2,0:T(8,128)(2,1)S(1)} %fusion.15), channel_id=1, replica_groups=mesh['grp'=2,'tp'=8,'sub'=2] {'tp'}, dimensions={0}, use_global_device_ids=true | all-gather | bytes 18432 | tf_op jit(solution)/shard_map/all_gather | solution.py:100
  175.2 30.6 %all-gather.5 = bf16[8,64,16]{1,2,0:T(8,128)(2,1)S(1)} all-gather(bf16[1,64,16]{1,2,0:T(8,128)(2,1)S(1)} %fusion.16), channel_id=1, replica_groups=mesh['grp'=2,'tp'=8,'sub'=2] {'tp'}, dimensions={0}, use_global_device_ids=true | all-gather | bytes 18432 | tf_op jit(solution)/shard_map/all_gather | solution.py:101
  205.9 9.3 %copy.83 = bf16[512,8,2,512]{3,1,2,0:T(8,128)(2,1)} copy(bf16[512,8,2,512]{3,2,1,0:T(2,128)(2,1)} %bitcast.90) | data formatting | bytes 16777216
  215.2 11.4 %copy.75 = bf16[1024,4096]{1,0:T(8,128)(2,1)} copy(bf16[1024,4096]{0,1:T(8,128)(2,1)} %bitcast.89) | data formatting | bytes 16777216 | tf_op jit(solution)/shard_map/dot_general | solution.py:143
  226.6 1.0 slice.26
  227.6 10.0 %while.19 = (s32[]{:T(128)}, f32[16,4,8]{0,2,1:T(8,128)S(1)}, f32[16,4,8]{0,2,1:T(8,128)S(1)}, f32[16,4,8,128]{3,2,1,0:T(8,128)S(1)}, f32[8,16,4,8]{1,3,2,0:T(8,...) while((s32[]{:T(128)}, f32[16,4,8]{0,2,1:T(8,128)S(1)}, ...), condition=%wide.region_4.5_spmd, body=%wide.region_3.4_spmd.sunk | while | flops 199685 | bytes 815255 | solution.py:23
  227.8 1.2 fusion.58
  229.2 1.2 fusion.58
  230.6 1.2 fusion.58
  232.0 1.2 fusion.58
  233.5 1.2 fusion.58
  234.9 1.2 fusion.58
  236.3 1.2 fusion.58
  238.2 6.3 %fusion.49 = f32[16,2,512]{2,0,1:T(8,128)} fusion(bf16[16,4096,1]{1,0,2:T(8,128)(2,1)S(1)} %reshape.199, bf16[2,512,4096]{2,1,0:T(8,128)(2,1)} %bitcast.88), kind=kOutput, calls=%fused_computation.77 | convolution fusion | flops 134217728 | bytes 8585216 | tf_op jit(solution)/shard_map/dot_general | solution.py:143
  244.6 8.6 %reduce-scatter.2.cloned.1.call-done = f32[16,1,512]{2,0,1:T(8,128)} async-done(((f32[16,2,512]{2,0,1:T(8,128)}), f32[16,1,512]{2,0,1:T(8,128)}) %reduce-scatter.2.cloned.1.call-update) | async-done | bytes 32784 | tf_op jit(solution)/shard_map/reduce_scatter | solution.py:147
  253.1 0.8 add_convert_fusion.1
  253.9 30.8 %all_gather.53 = bf16[16,1,4096]{2,0,1:T(8,128)(2,1)S(1)} all-gather(bf16[16,1,512]{2,0,1:T(8,128)(2,1)S(1)} %add_convert_fusion.1), channel_id=1, replica_groups=mesh['grp'=2,'tp'=8,'sub'=2] {'tp'}, dimensions={2}, use_global_device_ids=true | all-gather | bytes 147456 | tf_op jit(solution)/shard_map/all_gather | solution.py:48
  284.8 2.6 psum.21
  287.5 7.9 %fusion.7 = f32[16,1792]{1,0:T(8,128)} fusion(bf16[1,4096,1792]{2,1,0:T(8,128)(2,1)} %param.22, bf16[16,1,4096]{2,0,1:T(8,128)(2,1)S(1)} %all_gather.53, f32[4096]{0:T(1024)S(1)} %dynamic_slice.50, f32[16]{0:T(128)S(1)} %add_rsqrt_fusion), kind=kOutput, calls=%fused_computation.12 | convolution fusion | flops 235143168 | bytes 14942272 | tf_op jit(solution)/shard_map/dot_general | solution.py:157
  295.3 7.9 %fusion.5 = f32[16,1792]{1,0:T(8,128)} fusion(bf16[1,4096,1792]{2,1,0:T(8,128)(2,1)} %param.23, bf16[16,1,4096]{2,0,1:T(8,128)(2,1)S(1)} %all_gather.53, f32[4096]{0:T(1024)S(1)} %dynamic_slice.50, f32[16]{0:T(128)S(1)} %add_rsqrt_fusion), kind=kOutput, calls=%fused_computation.10 | convolution fusion | flops 235143168 | bytes 14942272 | tf_op jit(solution)/shard_map/dot_general | solution.py:160
  303.3 19.1 %all-reduce.3.cloned.1.call-done = (f32[16,1792]{1,0:T(8,128)}, f32[16,1792]{1,0:T(8,128)}) async-done(((f32[16,1792]{1,0:T(8,128)}, f32[16,1792]{1,0:T(8,128)}), (f32[16,1792]{1,0:T(8,128)}, f32[16,1792]{1,0:T(8,128)})) %all-reduce.3.cloned.1.call-update) | async-done | bytes 229392 | tf_op jit(solution)/shard_map/psum | solution.py:161
  322.4 8.1 %fusion.3 = f32[16,4096]{1,0:T(8,128)} fusion(bf16[1792,1,4096]{2,0,1:T(8,128)(2,1)} %param.24, f32[16,1792]{1,0:T(8,128)} %get-tuple-element.221, f32[16,1792]{1,0:T(8,128)} %get-tuple-element.222), kind=kOutput, calls=%fused_computation.8 | convolution fusion | flops 235053056 | bytes 15171584 | tf_op jit(solution)/shard_map/dot_general | solution.py:163
  330.6 50.5 %all-gather.11.cloned.1.call-done = f32[128,4096]{1,0:T(8,128)} async-done(((f32[16,4096]{1,0:T(8,128)}), f32[128,4096]{1,0:T(8,128)}) %all-gather.11.cloned.1.call-update) | async-done | bytes 2097168 | tf_op jit(solution)/shard_map/all_gather | solution.py:14
  381.0 1.7 reduce_sum.49
  (88 shorter events, 6.0 us)
Async XLA Ops:
  6.5 136.6 %copy-start = (bf16[8192,1,64]{0,2,1:T(8,128)(2,1)S(1)}, bf16[8192,1,64]{0,2,1:T(8,128)(2,1)}, u32[]{:S(2)}) copy-start(bf16[8192,1,64]{0,2,1:T(8,128)(2,1)} %param.18) | copy-start | bytes 3145732
  6.5 220.0 %all-gather.9.cloned.1.call-start = ((), (), s32[]{:S(2)}) async-start(), calls=%async_computation.2 | async-start | bytes 2359296 | tf_op jit(solution)/shard_map/all_gather | solution.py:18
  42.4 35.3 %copy-start.7 = (s32[16]{0:T(128)S(1)}, s32[16]{0:T(128)}, u32[]{:S(2)}) copy-start(s32[16]{0:T(128)} %param.27) | copy-start | bytes 196
  42.4 35.7 %copy-start.3 = (bf16[16,8,4,128]{3,2,1,0:T(4,128)(2,1)S(1)}, bf16[16,8,4,128]{3,2,1,0:T(4,128)(2,1)}, u32[]{:S(2)}) copy-start(bf16[16,8,4,128]{3,2,1,0:T(4,128)(2,1)} %param.25) | copy-start | bytes 393220
  42.4 36.0 %copy-start.4 = (bf16[16,8,4,128]{3,2,1,0:T(4,128)(2,1)S(1)}, bf16[16,8,4,128]{3,2,1,0:T(4,128)(2,1)}, u32[]{:S(2)}) copy-start(bf16[16,8,4,128]{3,2,1,0:T(4,128)(2,1)} %param.26) | copy-start | bytes 393220
  42.4 132.4 %copy-start.2 = (bf16[8192,1,64]{0,2,1:T(8,128)(2,1)S(1)}, bf16[8192,1,64]{0,2,1:T(8,128)(2,1)}, u32[]{:S(2)}) copy-start(bf16[8192,1,64]{0,2,1:T(8,128)(2,1)} %param.19) | copy-start | bytes 3145732
  79.8 173.4 %reduce-scatter.2.cloned.1.call-start = ((), (), s32[]{:S(2)}) async-start(), calls=%async_computation.1 | async-start | bytes 98304 | tf_op jit(solution)/shard_map/reduce_scatter | solution.py:147
  226.6 18.0 %copy-start.6 = (f32[8192]{0:T(1024)S(1)}, f32[8192]{0:T(1024)}, u32[]{:S(2)}) copy-start(f32[8192]{0:T(1024)} %param.21) | copy-start | bytes 98308
  226.6 26.6 %copy-start.5 = (bf16[16,1,512]{2,0,1:T(8,128)(2,1)S(1)}, bf16[16,1,512]{2,0,1:T(8,128)(2,1)}, u32[]{:S(2)}) copy-start(bf16[16,1,512]{2,0,1:T(8,128)(2,1)} %param.15) | copy-start | bytes 49156
  244.5 77.9 %all-reduce.3.cloned.1.call-start = ((), (), s32[]{:S(2)}) async-start(), calls=%async_computation.4 | async-start | bytes 458752 | tf_op jit(solution)/shard_map/psum | solution.py:161
  303.2 77.8 %all-gather.11.cloned.1.call-start = ((), (), s32[]{:S(2)}) async-start(), calls=%async_computation.3 | async-start | bytes 2359296 | tf_op jit(solution)/shard_map/all_gather | solution.py:14
  322.4 60.9 %copy-start.1 = (bf16[8192,1,64]{0,2,1:T(8,128)(2,1)S(1)}, bf16[8192,1,64]{0,2,1:T(8,128)(2,1)}, u32[]{:S(2)}) copy-start(bf16[8192,1,64]{0,2,1:T(8,128)(2,1)} %param.18) | copy-start | bytes 3145732
Sparse Core Ops, SparseCore 0:
  79.9 53.2 all-gather.8
  244.6 8.4 reduce-scatter.1
  303.4 19.0 all-reduce.2
  330.7 50.2 all-gather.10
